TPU v7x, 32 devices: a whole 2x2x4 slice. The times are simulated.
32 devices in a mesh: sweep: 4 (over z), layer: 8 (over y, x, core).
Axes of the slice: x: 2, y: 2, z: 4, core: 2. Of those that a mesh axis runs over, the one named last changes fastest.
Arguments:
- green: bfloat16 [4, 2, 8192, 8192], P('sweep', None, 'layer'), may hold values from -1 to 1
- down_source: float32 [4, 2, 16, 8192], P('sweep', None, None, 'layer'), may hold values from -6 to 6
- up_source: float32 [4, 2, 16, 8192], P('sweep', None, None, 'layer'), may hold values from -6 to 6
Outputs:
- total: float32 [4, 2, 16, 8192], P('sweep', None, None, 'layer')
All inputs are finite; a program needn't handle non-finite values.
Results may differ from a plain program's by a relative error of at most 0.02.
Values may be sent and summed in bfloat16 or wider, within the bound.
A program may use at most 64 MiB of HBM per device.

v0:
```python
import functools

import jax
import jax.numpy as jnp
from jax import lax
from jax.experimental import pallas as pl
from jax.experimental.pallas import tpu as pltpu
from jax.sharding import PartitionSpec as P

MESH = pl.DeviceIdType.MESH
F32, BF16 = jnp.float32, jnp.bfloat16
BY_LANES = (((1,), (1,)), ((), ()))


def turned(trace):
    half = trace.shape[0] // 2
    return jnp.concatenate([-trace[half:], trace[:half]], axis=0)


def rows_dot(trace, block):
    return lax.dot_general(trace, block, BY_LANES, preferred_element_type=F32)


def cols_dot(trace, block):
    return jnp.dot(trace, block, preferred_element_type=F32)


def sweeps(layers, peers, blocks, green, down_src, up_src, total,
           matrix, gathered, incoming, part_out, part_in, out_down, out_up, base, acc,
           load_sem, dsend, drecv, gsend, grecv, usend, urecv, psend, precv):
    z, j = lax.axis_index("sweep"), lax.axis_index("layer")
    own = down_src.shape[1]
    width = own // blocks
    odd = lax.rem(z, 2) == 1

    def span(k):
        return pl.ds(pl.multiple_of(k * width, width), width)

    def cols(i, k):
        return pl.ds(pl.multiple_of(i * own + k * width, width), width)

    def peer(d):
        return lax.rem(j + d, peers)

    def load(m, part):
        return pltpu.make_async_copy(
            green.at[part, span(m)], matrix.at[part, span(m)], load_sem.at[m, part])

    def wait_load(m):
        load(m, 0).wait()
        load(m, 1).wait()

    def remote(src, dst, send, recv, to):
        return pltpu.make_async_remote_copy(
            src_ref=src, dst_ref=dst, send_sem=send, recv_sem=recv, device_id=to, device_id_type=MESH)

    def pass_down(k):
        return remote(out_down.at[k], gathered.at[k, j], dsend.at[k], drecv.at[k], {"sweep": z + 1})

    def pass_up(k):
        return remote(out_up.at[k], incoming.at[k], usend.at[k], urecv.at[k], {"sweep": z - 1})

    def relay(k, d):
        return remote(gathered.at[k, j], gathered.at[k, j], gsend.at[k, d], grecv.at[k, j], {"layer": peer(d)})

    def relayed(k, d):
        i = peer(d)
        return remote(gathered.at[k, i], gathered.at[k, i], gsend.at[k, d], grecv.at[k, i], {"layer": i})

    def share(d, k):
        i = peer(d)
        return remote(part_out.at[i, k], part_in.at[j, k], psend.at[d, k], precv.at[j, k], {"layer": i})

    def shared(d, k):
        i = peer(d)
        return remote(part_out.at[i, k], part_in.at[i, k], psend.at[d, k], precv.at[i, k], {"layer": i})

    def share_all(d):
        i = peer(d)
        return remote(part_out.at[i], part_in.at[j], psend.at[d, 0], precv.at[j, 0], {"layer": i})

    def shared_all(d):
        i = peer(d)
        return remote(part_out.at[i], part_in.at[i], psend.at[d, 0], precv.at[i, 0], {"layer": i})

    for m in range(blocks):
        load(m, 0).start()
        load(m, 1).start()

    barrier = pltpu.get_barrier_semaphore()
    for d in range(1, peers):
        pl.semaphore_signal(barrier, inc=1, device_id={"layer": peer(d)}, device_id_type=MESH)
    for step in (1, layers - 1):
        pl.semaphore_signal(barrier, inc=1, device_id={"sweep": lax.rem(z + step, layers)}, device_id_type=MESH)
    pl.semaphore_wait(barrier, peers + 1)

    def finish_down(k, value):
        sum_of = up_src[:, span(k)] + value

        @pl.when(z < layers - 1)
        def _():
            base[:, span(k)] = sum_of
            out_down[k] = value.astype(BF16)
            pass_down(k).start()

        @pl.when(z == layers - 1)
        def _():
            total[:, span(k)] = sum_of
            out_up[k] = sum_of.astype(BF16)
            pass_up(k).start()

    def take(k):
        relayed_own = remote(
            out_down.at[k], gathered.at[k, j], dsend.at[k], drecv.at[k], {"sweep": z})
        relayed_own.wait_recv()
        for d in range(1, peers):
            relay(k, d).start()

    def wait_gather(k):
        for d in range(1, peers):
            relayed(k, d).wait_recv()

    def wait_up(k):
        remote(out_up.at[k], incoming.at[k], usend.at[k], urecv.at[k], {"sweep": z}).wait_recv()

    def down_term(m, ks):
        value = None
        for k in ks:
            for i in range(peers):
                trace = gathered[k, i]
                term = rows_dot(trace, matrix[0, span(m), cols(i, k)])
                value = term if value is None else value + term
                value = value + rows_dot(turned(trace), matrix[1, span(m), cols(i, k)])
        return value

    @pl.when(z == 0)
    def _():
        @pl.loop(0, blocks)
        def _(k):
            finish_down(k, down_src[:, span(k)])

        @pl.loop(0, blocks)
        def _(m):
            wait_load(m)

    @pl.when(z == 1)
    def _():
        @pl.loop(0, blocks)
        def _(k):
            take(k)

        @pl.loop(0, blocks)
        def _(k):
            wait_gather(k)

        @pl.loop(0, blocks)
        def _(m):
            wait_load(m)
            finish_down(m, down_src[:, span(m)] + down_term(m, range(blocks)))

    @pl.when(odd & (z > 1))
    def _():
        early = blocks // 2

        @pl.loop(0, blocks)
        def _(m):
            wait_load(m)

        base[...] = down_src[...]

        @pl.loop(0, blocks)
        def _(k):
            take(k)

        @pl.loop(0, early)
        def _(k):
            wait_gather(k)
            for m in range(blocks):
                base[:, span(m)] += down_term(m, [k])

        @pl.loop(early, blocks)
        def _(k):
            wait_gather(k)

        @pl.loop(0, blocks)
        def _(m):
            finish_down(m, base[:, span(m)] + down_term(m, range(early, blocks)))

    @pl.when(jnp.logical_not(odd) & (z > 0))
    def _():
        @pl.loop(0, blocks)
        def _(m):
            wait_load(m)

        base[...] = down_src[...]
        take(0)

        @pl.loop(0, blocks - 1)
        def _(k):
            take(k + 1)
            wait_gather(k)
            for m in range(blocks):
                base[:, span(m)] += down_term(m, [k])

        wait_gather(blocks - 1)
        for m in range(blocks):
            finish_down(m, base[:, span(m)] + down_term(m, [blocks - 1]))

    def finish_up(k):
        value = acc[j, :, span(k)]
        for d in range(1, peers):
            value = value + part_in[peer(d), k].astype(F32)
        value = base[:, span(k)] + value
        total[:, span(k)] = value

        @pl.when(z > 0)
        def _():
            out_up[k] = value.astype(BF16)
            pass_up(k).start()

    @pl.when(odd & (z < layers - 1))
    def _():
        @pl.loop(0, blocks)
        def _(k):
            wait_up(k)

        def reduce(k):
            for d in range(1, peers):
                shared(d, k).wait_recv()
            finish_up(k)

        @pl.loop(0, blocks)
        def _(k):
            for d in list(range(1, peers)) + [0]:
                i = peer(d)
                value = None
                for r in range(blocks):
                    trace = incoming[r]
                    term = cols_dot(trace, matrix[0, span(r), cols(i, k)])
                    value = term if value is None else value + term
                    value = value + cols_dot(turned(trace), matrix[1, span(r), cols(i, k)])
                if d:
                    part_out[i, k] = value.astype(BF16)
                else:
                    acc[i, :, span(k)] = value
            for d in range(1, peers):
                share(d, k).start()

            @pl.when(k > 0)
            def _():
                reduce(k - 1)

        reduce(blocks - 1)

        @pl.loop(0, blocks)
        def _(k):
            for d in range(1, peers):
                share(d, k).wait_send()

    @pl.when(jnp.logical_not(odd) & (z < layers - 1))
    def _():
        acc[...] = jnp.zeros_like(acc)

        def up_term(trace, r, i, k):
            value = cols_dot(trace, matrix[0, span(r), cols(i, k)])
            return value + cols_dot(turned(trace), matrix[1, span(r), cols(i, k)])

        @pl.loop(0, blocks - 1)
        def _(r):
            wait_up(r)
            trace = incoming[r]
            for i in range(peers):
                for k in range(blocks):
                    acc[i, :, span(k)] += up_term(trace, r, i, k)

        wait_up(blocks - 1)
        last = incoming[blocks - 1]
        for d in range(1, peers):
            i = peer(d)
            for k in range(blocks):
                value = acc[i, :, span(k)] + up_term(last, blocks - 1, i, k)
                part_out[i, k] = value.astype(BF16)
            share_all(d).start()
        for k in range(blocks):
            acc[j, :, span(k)] += up_term(last, blocks - 1, j, k)
        for d in range(1, peers):
            shared_all(d).wait_recv()

        @pl.loop(0, blocks)
        def _(k):
            finish_up(k)

        for d in range(1, peers):
            share_all(d).wait_send()

    @pl.when(z < layers - 1)
    def _():
        @pl.loop(0, blocks)
        def _(k):
            pass_down(k).wait_send()

    @pl.when(z > 0)
    def _():
        @pl.loop(0, blocks)
        def _(k):
            pass_up(k).wait_send()
            for d in range(1, peers):
                relay(k, d).wait_send()


def local(layers, peers, green, down_source, up_source):
    _one, parts, own, wide = green.shape
    sources = down_source.shape[2]
    both = parts * sources
    blocks = next(b for b in (4, 2, 1) if own % (b * 128) == 0)
    width = own // blocks
    vmem = pl.BlockSpec(memory_space=pltpu.VMEM)
    dma = pltpu.SemaphoreType.DMA
    result = pl.pallas_call(
        functools.partial(sweeps, layers, peers, blocks),
        out_shape=jax.ShapeDtypeStruct((both, own), F32),
        in_specs=[pl.BlockSpec(memory_space=pl.ANY), vmem, vmem],
        out_specs=vmem,
        scratch_shapes=[
            pltpu.VMEM((parts, own, wide), BF16),
            pltpu.VMEM((blocks, peers, both, width), BF16),
            pltpu.VMEM((blocks, both, width), BF16),
            pltpu.VMEM((peers, blocks, both, width), BF16),
            pltpu.VMEM((peers, blocks, both, width), BF16),
            pltpu.VMEM((blocks, both, width), BF16),
            pltpu.VMEM((blocks, both, width), BF16),
            pltpu.VMEM((both, own), F32),
            pltpu.VMEM((peers, both, own), F32),
            dma((blocks, 2)),
            dma((blocks,)), dma((blocks,)),
            dma((blocks, peers)), dma((blocks, peers)),
            dma((blocks,)), dma((blocks,)),
            dma((peers, blocks)), dma((peers, blocks)),
        ],
        compiler_params=pltpu.CompilerParams(
            collective_id=0, has_side_effects=True, vmem_limit_bytes=60 * 1024 * 1024),
    )(green[0], down_source.reshape(both, own), up_source.reshape(both, own))
    return result.reshape(1, parts, sources, own)


def solution(mesh):
    in_specs = (
        P("sweep", None, "layer", None),
        P("sweep", None, None, "layer"),
        P("sweep", None, None, "layer"),
    )
    out_specs = P("sweep", None, None, "layer")
    body = functools.partial(local, mesh.shape["sweep"], mesh.shape["layer"])
    return jax.shard_map(body, mesh=mesh, in_specs=in_specs, out_specs=out_specs, check_vma=False)
```

profile of v0, /device:TPU:0, one launch (start us, length us, event | category | flops | bytes accessed | tf_op | source)
XLA Modules:
  0.0 90.2 jit_solution(9804455752208697594)
XLA Ops:
  0.0 88.6 %shard_map.37 = f32[32,1024]{1,0:T(8,128)} custom-call(bf16[2,1024,8192]{2,1,0:T(8,128)(2,1)} %bitcast.4, f32[32,1024]{1,0:T(8,128)} %bitcast.6, f32[32,1024]{1,0:T(8,128)} %bitcast.7), custom_call_target="tpu_custom_call" | custom-call | tf_op jit(solution)/shard_map/pallas_call | solution.py:319
  88.6 1.6 %copy.5 = f32[1,2,16,1024]{3,2,1,0:T(8,128)} copy(f32[1,2,16,1024]{3,2,1,0:T(8,128)} %bitcast.5) | data formatting | bytes 262144
where the time goes:
time: 90.6 us; the launch traced here: 90.2 us
  Pallas kernels  88.6 us (98%)
  local copies, waits for them, and re-layouts  1.57 us (2%)
    pallas_call x1, Pallas kernels, local(): pl.pallas_call(functools.partial(sweeps, layers, peers, blocks), out_shap...  88.6 us

commit v1 on v0

v1 whole, which is shorter than its diff:
```python
import functools

import jax
import jax.numpy as jnp
from jax import lax
from jax.experimental import pallas as pl
from jax.experimental.pallas import tpu as pltpu
from jax.sharding import PartitionSpec as P

MESH = pl.DeviceIdType.MESH
F32, BF16 = jnp.float32, jnp.bfloat16
GROUPS = 4


def turned(trace):
    half = trace.shape[0] // 2
    return jnp.concatenate([-trace[half:], trace[:half]], axis=0)


def dot(trace, block):
    return jnp.dot(trace, block, preferred_element_type=F32)


def sweeps(layers, peers, blocks, green, down_hbm, up_hbm, total,
           matrix, down_src, up_src, gathered, incoming, part_out, part_in, out_down, out_up, base, acc,
           src_sem, load_sem, dsend, drecv, gsend, grecv, usend, urecv, psend, precv):
    z, j = lax.axis_index("sweep"), lax.axis_index("layer")
    own = down_src.shape[1]
    width = own // blocks
    groups = min(GROUPS, peers)
    per = peers // groups
    odd = lax.rem(z, 2) == 1

    def span(k):
        return pl.ds(pl.multiple_of(k * width, width), width)

    def cols(i, k):
        return pl.ds(pl.multiple_of(i * own + k * width, width), width)

    def peer(d):
        i, bit = j, 1
        while bit < peers:
            if d & bit:
                i = i + bit - 2 * bit * lax.rem(j // bit, 2)
            bit *= 2
        return i

    others = range(peers - 1, 0, -1)

    def load(m, part, g):
        at = (part, span(m), pl.ds(g * per * own, per * own))
        return pltpu.make_async_copy(green.at[at], matrix.at[at], load_sem.at[m, part, g])

    def start_loads():
        for m in range(blocks):
            for g in range(groups):
                for part in (0, 1):
                    load(m, part, g).start()

    def wait_load(m):
        for g in range(groups):
            for part in (0, 1):
                load(m, part, g).wait()

    sources = [pltpu.make_async_copy(down_hbm, down_src, src_sem.at[0]),
               pltpu.make_async_copy(up_hbm, up_src, src_sem.at[1])]

    def remote(src, dst, send, recv, to):
        return pltpu.make_async_remote_copy(
            src_ref=src, dst_ref=dst, send_sem=send, recv_sem=recv, device_id=to, device_id_type=MESH)

    def pass_down(k):
        return remote(out_down.at[k], gathered.at[k, j], dsend.at[k], drecv.at[k], {"sweep": z + 1})

    def pass_up(k):
        return remote(out_up.at[k], incoming.at[k], usend.at[k], urecv.at[k], {"sweep": z - 1})

    def relay(k, d):
        return remote(gathered.at[k, j], gathered.at[k, j], gsend.at[k, d], grecv.at[k, j], {"layer": peer(d)})

    def relayed(k, d):
        i = peer(d)
        return remote(gathered.at[k, i], gathered.at[k, i], gsend.at[k, d], grecv.at[k, i], {"layer": i})

    def share(d, k):
        i = peer(d)
        return remote(part_out.at[i, k], part_in.at[j, k], psend.at[d, k], precv.at[j, k], {"layer": i})

    def shared(d, k):
        i = peer(d)
        return remote(part_out.at[i, k], part_in.at[i, k], psend.at[d, k], precv.at[i, k], {"layer": i})

    @pl.when(z > 0)
    def _():
        start_loads()

    for copy in sources:
        copy.start()

    barrier = pltpu.get_barrier_semaphore()
    for d in others:
        pl.semaphore_signal(barrier, inc=1, device_id={"layer": peer(d)}, device_id_type=MESH)
    for step in (1, layers - 1):
        pl.semaphore_signal(barrier, inc=1, device_id={"sweep": lax.rem(z + step, layers)}, device_id_type=MESH)

    def take(k):
        remote(out_down.at[k], gathered.at[k, j], dsend.at[k], drecv.at[k], {"sweep": z}).wait_recv()
        for d in others:
            relay(k, d).start()

    def flip(m, g):
        for part in (0, 1):
            load(m, part, g).wait()
        for i in range(g * per, (g + 1) * per):
            for k in range(blocks):
                for part in (0, 1):
                    at = (part, span(m), cols(i, k))
                    matrix[at] = matrix[at].T

    @pl.when(z > 0)
    def _():
        for g in range(groups):
            flip(0, g)

    pl.semaphore_wait(barrier, peers + 1)

    def finish_down(k, value, last):
        sum_of = up_src[:, span(k)] + value

        def go_on():
            base[:, span(k)] = sum_of
            out_down[k] = value.astype(BF16)
            pass_down(k).start()

        def turn_back():
            total[:, span(k)] = sum_of
            out_up[k] = sum_of.astype(BF16)
            pass_up(k).start()

        if last is None:
            pl.when(z < layers - 1)(go_on)
            pl.when(z == layers - 1)(turn_back)
        elif last:
            turn_back()
        else:
            go_on()

    even_last = None if layers % 2 else False
    odd_last = True if layers == 4 else None

    def wait_gather(k):
        for d in others:
            relayed(k, d).wait_recv()

    def down_term(m, ks):
        value = None
        for k in ks:
            for i in range(peers):
                trace = gathered[k, i]
                term = dot(trace, matrix[0, span(m), cols(i, k)])
                value = term if value is None else value + term
                value = value + dot(turned(trace), matrix[1, span(m), cols(i, k)])
        return value

    def again():
        @pl.when(z < layers - 1)
        def _():
            start_loads()

    def wait_sources():
        for copy in sources:
            copy.wait()

    @pl.when(z == 0)
    def _():
        wait_sources()

        @pl.loop(0, blocks)
        def _(k):
            finish_down(k, down_src[:, span(k)], False)

        start_loads()

    @pl.when(z > 0)
    def _():
        @pl.loop(1, blocks)
        def _(m):
            for g in range(groups):
                flip(m, g)
                if g == 0:
                    @pl.when((z == 1) & (m == blocks // 2))
                    def _():
                        @pl.loop(0, blocks)
                        def _(k):
                            take(k)
        wait_sources()

    @pl.when(z == 1)
    def _():
        @pl.loop(0, blocks)
        def _(k):
            wait_gather(k)

        @pl.loop(0, blocks)
        def _(m):
            finish_down(m, down_src[:, span(m)] + down_term(m, range(blocks)), False)

        again()

    @pl.when(odd & (z > 1))
    def _():
        early = blocks // 2
        base[...] = down_src[...]

        @pl.loop(0, blocks)
        def _(k):
            take(k)

        @pl.loop(0, early)
        def _(k):
            wait_gather(k)
            for m in range(blocks):
                base[:, span(m)] += down_term(m, [k])

        @pl.loop(early, blocks)
        def _(k):
            wait_gather(k)

        @pl.loop(0, blocks)
        def _(m):
            finish_down(m, base[:, span(m)] + down_term(m, range(early, blocks)), odd_last)

        again()

    @pl.when(jnp.logical_not(odd) & (z > 0))
    def _():
        base[...] = down_src[...]
        take(0)

        @pl.loop(0, blocks - 1)
        def _(k):
            take(k + 1)
            wait_gather(k)
            for m in range(blocks):
                base[:, span(m)] += down_term(m, [k])

        wait_gather(blocks - 1)
        for m in range(blocks):
            finish_down(m, base[:, span(m)] + down_term(m, [blocks - 1]), even_last)

        again()

    def wait_up(k):
        remote(out_up.at[k], incoming.at[k], usend.at[k], urecv.at[k], {"sweep": z}).wait_recv()

    def up_term(i, k, rs):
        value = None
        for r in rs:
            trace = incoming[r]
            term = dot(trace, matrix[0, span(r), cols(i, k)])
            value = term if value is None else value + term
            value = value + dot(turned(trace), matrix[1, span(r), cols(i, k)])
        return value

    def finish_up(k):
        value = acc[j, :, span(k)]
        for d in range(1, peers):
            value = value + part_in[peer(d), k].astype(F32)
        value = base[:, span(k)] + value
        total[:, span(k)] = value

        @pl.when(z > 0)
        def _():
            out_up[k] = value.astype(BF16)
            pass_up(k).start()

    def up(early):
        acc[...] = jnp.zeros_like(acc)

        @pl.loop(0, early)
        def _(r):
            wait_load(r)
            wait_up(r)
            for i in range(peers):
                for k in range(blocks):
                    acc[i, :, span(k)] += up_term(i, k, [r])

        @pl.loop(early, blocks)
        def _(r):
            wait_load(r)
            wait_up(r)

        late = range(early, blocks)

        @pl.loop(0, blocks)
        def _(k):
            for d in others:
                i = peer(d)
                part_out[i, k] = (acc[i, :, span(k)] + up_term(i, k, late)).astype(BF16)
            for d in others:
                share(d, k).start()

        for k in range(blocks):
            acc[j, :, span(k)] += up_term(j, k, late)

        @pl.loop(0, blocks)
        def _(k):
            for d in others:
                shared(d, k).wait_recv()
            finish_up(k)

        @pl.loop(0, blocks)
        def _(k):
            for d in others:
                share(d, k).wait_send()

    @pl.when(odd & (z < layers - 1))
    def _():
        up(blocks // 2)

    @pl.when(jnp.logical_not(odd) & (z < layers - 1))
    def _():
        up(blocks - 1)

    @pl.when(z < layers - 1)
    def _():
        @pl.loop(0, blocks)
        def _(k):
            pass_down(k).wait_send()

    @pl.when(z > 0)
    def _():
        @pl.loop(0, blocks)
        def _(k):
            pass_up(k).wait_send()
            for d in others:
                relay(k, d).wait_send()


def local(layers, peers, green, down_source, up_source):
    _one, parts, own, wide = green.shape
    sources = down_source.shape[2]
    both = parts * sources
    width = next(w for w in (256, 128) if own % w == 0)
    blocks = own // width
    groups = min(GROUPS, peers)
    vmem = pl.BlockSpec(memory_space=pltpu.VMEM)
    dma = pltpu.SemaphoreType.DMA
    result = pl.pallas_call(
        functools.partial(sweeps, layers, peers, blocks),
        out_shape=pltpu.VMEM((both, own), F32),
        in_specs=[pl.BlockSpec(memory_space=pltpu.HBM)] * 3,
        out_specs=vmem,
        scratch_shapes=[
            pltpu.VMEM((parts, own, wide), BF16),
            pltpu.VMEM((both, own), F32),
            pltpu.VMEM((both, own), F32),
            pltpu.VMEM((blocks, peers, both, width), BF16),
            pltpu.VMEM((blocks, both, width), BF16),
            pltpu.VMEM((peers, blocks, both, width), BF16),
            pltpu.VMEM((peers, blocks, both, width), BF16),
            pltpu.VMEM((blocks, both, width), BF16),
            pltpu.VMEM((blocks, both, width), BF16),
            pltpu.VMEM((both, own), F32),
            pltpu.VMEM((peers, both, own), F32),
            dma((2,)),
            dma((blocks, 2, groups)),
            dma((blocks,)), dma((blocks,)),
            dma((blocks, peers)), dma((blocks, peers)),
            dma((blocks,)), dma((blocks,)),
            dma((peers, blocks)), dma((peers, blocks)),
        ],
        compiler_params=pltpu.CompilerParams(
            collective_id=0, has_side_effects=True, vmem_limit_bytes=60 * 1024 * 1024),
    )(green[0], down_source.reshape(both, own), up_source.reshape(both, own))
    return result.reshape(1, parts, sources, own)


def solution(mesh):
    in_specs = (
        P("sweep", None, "layer", None),
        P("sweep", None, None, "layer"),
        P("sweep", None, None, "layer"),
    )
    out_specs = P("sweep", None, None, "layer")
    body = functools.partial(local, mesh.shape["sweep"], mesh.shape["layer"])
    return jax.shard_map(body, mesh=mesh, in_specs=in_specs, out_specs=out_specs, check_vma=False)
```

time: 90.6 us -> 83.6 us (0.923)
  Pallas kernels: 88.6 us -> 82.8 us
  local copies, waits for them, and re-layouts: 1.57 us -> 0.66 us
    pallas_call x1, Pallas kernels: 88.6 us -> 82.8 us  [local(): pl.pallas_call(functools.partial(sweeps, layers, peers, blocks), out_shap...]
    unnamed x1, local copies, waits for them, and re-layouts: 1.57 us -> 0.66 us
where the time goes in v1:
time: 83.6 us; the launch traced here: 83.5 us
  Pallas kernels  82.8 us (99%)
    pallas_call x1, Pallas kernels, local(): pl.pallas_call(functools.partial(sweeps, layers, peers, blocks), out_shap...  82.8 us

profile of v1, /device:TPU:0, one launch (start us, length us, event | category | flops | bytes accessed | tf_op | source)
XLA Modules:
  0.0 83.5 jit_solution(11560650336944530581)
XLA Ops:
  0.0 82.8 %shard_map.37 = f32[32,1024]{1,0:T(8,128)S(1)} custom-call(bf16[2,1024,8192]{2,1,0:T(8,128)(2,1)} %bitcast.5, f32[32,1024]{1,0:T(8,128)} %bitcast.6, f32[32,1024]{1,0:T(8,128)} %bitcast.7), custom_call_target="tpu_custom_call" | custom-call | tf_op jit(solution)/shard_map/pallas_call | solution.py:349
  82.8 0.7 copy.5

commit v2 on v1

--- a/solution.py
+++ b/solution.py
@@ -10,6 +10,7 @@
 MESH = pl.DeviceIdType.MESH
 F32, BF16 = jnp.float32, jnp.bfloat16
 GROUPS = 4
+EARLY = 1
 
 
 def turned(trace):
@@ -22,8 +23,8 @@
 
 
 def sweeps(layers, peers, blocks, green, down_hbm, up_hbm, total,
-           matrix, down_src, up_src, gathered, incoming, part_out, part_in, out_down, out_up, base, acc,
-           src_sem, load_sem, dsend, drecv, gsend, grecv, usend, urecv, psend, precv):
+           matrix, down_src, up_src, gathered, incoming, pair_out, pair_in, part_out, part_in, out_down, out_up, base, acc,
+           src_sem, load_sem, dsend, drecv, gsend, grecv, fsend, usend, urecv, xsend, xrecv, psend, precv):
     z, j = lax.axis_index("sweep"), lax.axis_index("layer")
     own = down_src.shape[1]
     width = own // blocks
@@ -46,21 +47,22 @@
         return i
 
     others = range(peers - 1, 0, -1)
-
-    def load(m, part, g):
-        at = (part, span(m), pl.ds(g * per * own, per * own))
-        return pltpu.make_async_copy(green.at[at], matrix.at[at], load_sem.at[m, part, g])
+    far = [d for d in others if bin(d // 2).count("1") > 1]
+    near = [d for d in others if d not in far]
+    halves = range(peers // 2 - 1, 0, -1)
+
+    def load(m, g):
+        at = (slice(None), span(m), pl.ds(g * per * own, per * own))
+        return pltpu.make_async_copy(green.at[at], matrix.at[at], load_sem.at[m, g])
 
     def start_loads():
         for m in range(blocks):
             for g in range(groups):
-                for part in (0, 1):
-                    load(m, part, g).start()
+                load(m, g).start()
 
     def wait_load(m):
         for g in range(groups):
-            for part in (0, 1):
-                load(m, part, g).wait()
+            load(m, g).wait()
 
     sources = [pltpu.make_async_copy(down_hbm, down_src, src_sem.at[0]),
                pltpu.make_async_copy(up_hbm, up_src, src_sem.at[1])]
@@ -70,25 +72,23 @@
             src_ref=src, dst_ref=dst, send_sem=send, recv_sem=recv, device_id=to, device_id_type=MESH)
 
     def pass_down(k):
-        return remote(out_down.at[k], gathered.at[k, j], dsend.at[k], drecv.at[k], {"sweep": z + 1})
+        return remote(out_down.at[k], gathered.at[k, j], dsend, drecv.at[k], {"sweep": z + 1})
+
+    def pass_far(k, d):
+        return remote(out_down.at[k], gathered.at[k, j], fsend, grecv.at[k],
+                      {"sweep": z + 1, "layer": peer(d)})
 
     def pass_up(k):
-        return remote(out_up.at[k], incoming.at[k], usend.at[k], urecv.at[k], {"sweep": z - 1})
+        return remote(out_up.at[k], incoming.at[k], usend, urecv.at[k], {"sweep": z - 1})
 
     def relay(k, d):
-        return remote(gathered.at[k, j], gathered.at[k, j], gsend.at[k, d], grecv.at[k, j], {"layer": peer(d)})
-
-    def relayed(k, d):
-        i = peer(d)
-        return remote(gathered.at[k, i], gathered.at[k, i], gsend.at[k, d], grecv.at[k, i], {"layer": i})
-
-    def share(d, k):
-        i = peer(d)
-        return remote(part_out.at[i, k], part_in.at[j, k], psend.at[d, k], precv.at[j, k], {"layer": i})
-
-    def shared(d, k):
-        i = peer(d)
-        return remote(part_out.at[i, k], part_in.at[i, k], psend.at[d, k], precv.at[i, k], {"layer": i})
+        return remote(gathered.at[k, j], gathered.at[k, j], gsend, grecv.at[k], {"layer": peer(d)})
+
+    def swap(k):
+        return remote(pair_out.at[k], pair_in.at[k], xsend, xrecv.at[k], {"layer": peer(1)})
+
+    def share(h, k):
+        return remote(part_out.at[k, h], part_in.at[k, h], psend, precv.at[k], {"layer": peer(2 * h)})
 
     @pl.when(z > 0)
     def _():
@@ -98,19 +98,27 @@
         copy.start()
 
     barrier = pltpu.get_barrier_semaphore()
-    for d in others:
-        pl.semaphore_signal(barrier, inc=1, device_id={"layer": peer(d)}, device_id_type=MESH)
-    for step in (1, layers - 1):
-        pl.semaphore_signal(barrier, inc=1, device_id={"sweep": lax.rem(z + step, layers)}, device_id_type=MESH)
+    def sent(sources_of, sem):
+        remote(sources_of, sources_of, sem, sem, {"sweep": z}).wait_send()
+
+    def greet(to):
+        pl.semaphore_signal(barrier, inc=1, device_id=to, device_id_type=MESH)
+
+    @pl.when(z > 0)
+    def _():
+        greet({"sweep": z - 1})
+        for d in far:
+            greet({"sweep": z - 1, "layer": peer(d)})
+        for d in others:
+            greet({"layer": peer(d)})
 
     def take(k):
-        remote(out_down.at[k], gathered.at[k, j], dsend.at[k], drecv.at[k], {"sweep": z}).wait_recv()
-        for d in others:
+        remote(out_down.at[k], gathered.at[k, j], dsend, drecv.at[k], {"sweep": z}).wait_recv()
+        for d in near:
             relay(k, d).start()
 
     def flip(m, g):
-        for part in (0, 1):
-            load(m, part, g).wait()
+        load(m, g).wait()
         for i in range(g * per, (g + 1) * per):
             for k in range(blocks):
                 for part in (0, 1):
@@ -122,7 +130,17 @@
         for g in range(groups):
             flip(0, g)
 
-    pl.semaphore_wait(barrier, peers + 1)
+    @pl.when(z == 0)
+    def _():
+        pl.semaphore_wait(barrier, 1 + len(far))
+
+    @pl.when((z > 0) & (z < layers - 1))
+    def _():
+        pl.semaphore_wait(barrier, peers + len(far))
+
+    @pl.when(z == layers - 1)
+    def _():
+        pl.semaphore_wait(barrier, peers - 1)
 
     def finish_down(k, value, last):
         sum_of = up_src[:, span(k)] + value
@@ -130,6 +148,8 @@
         def go_on():
             base[:, span(k)] = sum_of
             out_down[k] = value.astype(BF16)
+            for d in far:
+                pass_far(k, d).start()
             pass_down(k).start()
 
         def turn_back():
@@ -149,8 +169,8 @@
     odd_last = True if layers == 4 else None
 
     def wait_gather(k):
-        for d in others:
-            relayed(k, d).wait_recv()
+        rest = gathered.at[k, pl.ds(0, peers - 1)]
+        remote(rest, rest, gsend, grecv.at[k], {"sweep": z}).wait_recv()
 
     def down_term(m, ks):
         value = None
@@ -187,10 +207,10 @@
         def _(m):
             for g in range(groups):
                 flip(m, g)
-                if g == 0:
+                if g % 2 == 1:
                     @pl.when((z == 1) & (m == blocks // 2))
                     def _():
-                        @pl.loop(0, blocks)
+                        @pl.loop(g // 2 * blocks // 2, (g // 2 + 1) * blocks // 2)
                         def _(k):
                             take(k)
         wait_sources()
@@ -209,7 +229,7 @@
 
     @pl.when(odd & (z > 1))
     def _():
-        early = blocks // 2
+        early = EARLY
         base[...] = down_src[...]
 
         @pl.loop(0, blocks)
@@ -235,12 +255,17 @@
     @pl.when(jnp.logical_not(odd) & (z > 0))
     def _():
         base[...] = down_src[...]
-        take(0)
+        for k in range(min(2, blocks)):
+            take(k)
 
         @pl.loop(0, blocks - 1)
         def _(k):
-            take(k + 1)
             wait_gather(k)
+
+            @pl.when(k + 2 < blocks)
+            def _():
+                take(k + 2)
+
             for m in range(blocks):
                 base[:, span(m)] += down_term(m, [k])
 
@@ -251,7 +276,7 @@
         again()
 
     def wait_up(k):
-        remote(out_up.at[k], incoming.at[k], usend.at[k], urecv.at[k], {"sweep": z}).wait_recv()
+        remote(out_up.at[k], incoming.at[k], usend, urecv.at[k], {"sweep": z}).wait_recv()
 
     def up_term(i, k, rs):
         value = None
@@ -264,8 +289,8 @@
 
     def finish_up(k):
         value = acc[j, :, span(k)]
-        for d in range(1, peers):
-            value = value + part_in[peer(d), k].astype(F32)
+        for h in halves:
+            value = value + part_in[k, h].astype(F32)
         value = base[:, span(k)] + value
         total[:, span(k)] = value
 
@@ -274,7 +299,16 @@
             out_up[k] = value.astype(BF16)
             pass_up(k).start()
 
-    def up(early):
+    def combine(k):
+        swap(k).wait_recv()
+        for h in halves:
+            i = peer(2 * h)
+            part_out[k, h] = (acc[i, :, span(k)] + pair_in[k, h].astype(F32)).astype(BF16)
+        for h in halves:
+            share(h, k).start()
+        acc[j, :, span(k)] += pair_in[k, 0].astype(F32)
+
+    def up(early, step):
         acc[...] = jnp.zeros_like(acc)
 
         @pl.loop(0, early)
@@ -292,49 +326,57 @@
 
         late = range(early, blocks)
 
-        @pl.loop(0, blocks)
-        def _(k):
-            for d in others:
+        def hand_over(k):
+            for d in range(peers - 1, 0, -2):
                 i = peer(d)
-                part_out[i, k] = (acc[i, :, span(k)] + up_term(i, k, late)).astype(BF16)
-            for d in others:
-                share(d, k).start()
-
-        for k in range(blocks):
-            acc[j, :, span(k)] += up_term(j, k, late)
-
-        @pl.loop(0, blocks)
-        def _(k):
-            for d in others:
-                shared(d, k).wait_recv()
+                pair_out[k, d // 2] = (acc[i, :, span(k)] + up_term(i, k, late)).astype(BF16)
+
+        def keep(k):
+            for d in range(peers - 2, -1, -2):
+                i = peer(d)
+                acc[i, :, span(k)] += up_term(i, k, late)
+
+        @pl.loop(0, blocks // step)
+        def _(c):
+            for n in range(step):
+                hand_over(c * step + n)
+            for n in range(step):
+                swap(c * step + n).start()
+
+        @pl.loop(0, blocks // step)
+        def _(c):
+            for n in range(step):
+                keep(c * step + n)
+            for n in range(step):
+                combine(c * step + n)
+
+        @pl.loop(0, blocks)
+        def _(k):
+            shares = pl.ds(0, len(halves))
+            remote(part_out.at[k, shares], part_in.at[k, shares], psend, precv.at[k], {"sweep": z}).wait_recv()
             finish_up(k)
 
-        @pl.loop(0, blocks)
-        def _(k):
-            for d in others:
-                share(d, k).wait_send()
+        sent(pair_out, xsend)
+        sent(part_out.at[:, pl.ds(0, len(halves))], psend)
 
     @pl.when(odd & (z < layers - 1))
     def _():
-        up(blocks // 2)
+        up(blocks // 2, 1)
 
     @pl.when(jnp.logical_not(odd) & (z < layers - 1))
     def _():
-        up(blocks - 1)
+        up(blocks - 1, 2)
 
     @pl.when(z < layers - 1)
     def _():
-        @pl.loop(0, blocks)
-        def _(k):
-            pass_down(k).wait_send()
+        sent(out_down, dsend)
+        if far:
+            sent(gathered.at[:, pl.ds(0, len(far))], fsend)
 
     @pl.when(z > 0)
     def _():
-        @pl.loop(0, blocks)
-        def _(k):
-            pass_up(k).wait_send()
-            for d in others:
-                relay(k, d).wait_send()
+        sent(out_up, usend)
+        sent(gathered.at[:, pl.ds(0, len(near))], gsend)
 
 
 def local(layers, peers, green, down_source, up_source):
@@ -357,18 +399,22 @@
             pltpu.VMEM((both, own), F32),
             pltpu.VMEM((blocks, peers, both, width), BF16),
             pltpu.VMEM((blocks, both, width), BF16),
-            pltpu.VMEM((peers, blocks, both, width), BF16),
-            pltpu.VMEM((peers, blocks, both, width), BF16),
+            pltpu.VMEM((blocks, peers // 2, both, width), BF16),
+            pltpu.VMEM((blocks, peers // 2, both, width), BF16),
+            pltpu.VMEM((blocks, peers // 2, both, width), BF16),
+            pltpu.VMEM((blocks, peers // 2, both, width), BF16),
             pltpu.VMEM((blocks, both, width), BF16),
             pltpu.VMEM((blocks, both, width), BF16),
             pltpu.VMEM((both, own), F32),
             pltpu.VMEM((peers, both, own), F32),
             dma((2,)),
-            dma((blocks, 2, groups)),
-            dma((blocks,)), dma((blocks,)),
-            dma((blocks, peers)), dma((blocks, peers)),
-            dma((blocks,)), dma((blocks,)),
-            dma((peers, blocks)), dma((peers, blocks)),
+            dma((blocks, groups)),
+            dma(()), dma((blocks,)),
+            dma(()), dma((blocks,)),
+            dma(()),
+            dma(()), dma((blocks,)),
+            dma(()), dma((blocks,)),
+            dma(()), dma((blocks,)),
         ],
         compiler_params=pltpu.CompilerParams(
             collective_id=0, has_side_effects=True, vmem_limit_bytes=60 * 1024 * 1024),

time: 83.6 us -> 78.3 us (0.937)
  Pallas kernels: 82.8 us -> 77.5 us
    pallas_call x1, Pallas kernels: 82.8 us -> 77.5 us  [local(): pl.pallas_call(functools.partial(sweeps, layers, peers, blocks), out_shap...]
where the time goes in v2:
time: 78.3 us; the launch traced here: 78.2 us
  Pallas kernels  77.5 us (99%)
    pallas_call x1, Pallas kernels, local(): pl.pallas_call(functools.partial(sweeps, layers, peers, blocks), out_shap...  77.5 us

profile of v2, /device:TPU:0, one launch (start us, length us, event | category | flops | bytes accessed | tf_op | source)
XLA Modules:
  0.0 78.2 jit_solution(14361441463758400223)
XLA Ops:
  0.0 77.5 %shard_map.37 = f32[32,1024]{1,0:T(8,128)S(1)} custom-call(bf16[2,1024,8192]{2,1,0:T(8,128)(2,1)} %bitcast.5, f32[32,1024]{1,0:T(8,128)} %bitcast.6, f32[32,1024]{1,0:T(8,128)} %bitcast.7), custom_call_target="tpu_custom_call" | custom-call | tf_op jit(solution)/shard_map/pallas_call | solution.py:391
  77.5 0.7 copy.5

commit v3 on v2

--- a/solution.py
+++ b/solution.py
@@ -10,7 +10,8 @@
 MESH = pl.DeviceIdType.MESH
 F32, BF16 = jnp.float32, jnp.bfloat16
 GROUPS = 4
-EARLY = 1
+EARLY = 3
+AHEAD = 1
 
 
 def turned(trace):
@@ -24,7 +25,7 @@
 
 def sweeps(layers, peers, blocks, green, down_hbm, up_hbm, total,
            matrix, down_src, up_src, gathered, incoming, pair_out, pair_in, part_out, part_in, out_down, out_up, base, acc,
-           src_sem, load_sem, dsend, drecv, gsend, grecv, fsend, usend, urecv, xsend, xrecv, psend, precv):
+           src_sem, load_sem, dsend, drecv, gsend, grecv, fsend, frecv, usend, urecv, xsend, xrecv, psend, precv):
     z, j = lax.axis_index("sweep"), lax.axis_index("layer")
     own = down_src.shape[1]
     width = own // blocks
@@ -49,6 +50,7 @@
     others = range(peers - 1, 0, -1)
     far = [d for d in others if bin(d // 2).count("1") > 1]
     near = [d for d in others if d not in far]
+    soon, later = [0, 1] + far, [d for d in near if d > 1]
     halves = range(peers // 2 - 1, 0, -1)
 
     def load(m, g):
@@ -75,14 +77,15 @@
         return remote(out_down.at[k], gathered.at[k, j], dsend, drecv.at[k], {"sweep": z + 1})
 
     def pass_far(k, d):
-        return remote(out_down.at[k], gathered.at[k, j], fsend, grecv.at[k],
+        return remote(out_down.at[k], gathered.at[k, j], fsend, frecv.at[k],
                       {"sweep": z + 1, "layer": peer(d)})
 
     def pass_up(k):
         return remote(out_up.at[k], incoming.at[k], usend, urecv.at[k], {"sweep": z - 1})
 
     def relay(k, d):
-        return remote(gathered.at[k, j], gathered.at[k, j], gsend, grecv.at[k], {"layer": peer(d)})
+        return remote(gathered.at[k, j], gathered.at[k, j], gsend, (frecv if d == 1 else grecv).at[k],
+                      {"layer": peer(d)})
 
     def swap(k):
         return remote(pair_out.at[k], pair_in.at[k], xsend, xrecv.at[k], {"layer": peer(1)})
@@ -168,14 +171,25 @@
     even_last = None if layers % 2 else False
     odd_last = True if layers == 4 else None
 
+    def wait_some(k, count, sem):
+        if count:
+            some = gathered.at[k, pl.ds(0, count)]
+            remote(some, some, gsend, sem.at[k], {"sweep": z}).wait_recv()
+
+    def wait_soon(k):
+        wait_some(k, len(soon) - 1, frecv)
+
+    def wait_later(k):
+        wait_some(k, len(later), grecv)
+
     def wait_gather(k):
-        rest = gathered.at[k, pl.ds(0, peers - 1)]
-        remote(rest, rest, gsend, grecv.at[k], {"sweep": z}).wait_recv()
-
-    def down_term(m, ks):
-        value = None
-        for k in ks:
-            for i in range(peers):
+        wait_soon(k)
+        wait_later(k)
+
+    def down_term(m, pairs):
+        value = jnp.zeros((down_src.shape[0], width), F32) if not pairs else None
+        for k, ds in pairs:
+            for i in (range(peers) if ds is None else map(peer, ds)):
                 trace = gathered[k, i]
                 term = dot(trace, matrix[0, span(m), cols(i, k)])
                 value = term if value is None else value + term
@@ -207,7 +221,7 @@
         def _(m):
             for g in range(groups):
                 flip(m, g)
-                if g % 2 == 1:
+                if g % 2 == 0:
                     @pl.when((z == 1) & (m == blocks // 2))
                     def _():
                         @pl.loop(g // 2 * blocks // 2, (g // 2 + 1) * blocks // 2)
@@ -223,13 +237,13 @@
 
         @pl.loop(0, blocks)
         def _(m):
-            finish_down(m, down_src[:, span(m)] + down_term(m, range(blocks)), False)
+            finish_down(m, down_src[:, span(m)] + down_term(m, [(k, None) for k in range(blocks)]), False)
 
         again()
 
     @pl.when(odd & (z > 1))
     def _():
-        early = EARLY
+        early = min(EARLY, blocks)
         base[...] = down_src[...]
 
         @pl.loop(0, blocks)
@@ -238,40 +252,59 @@
 
         @pl.loop(0, early)
         def _(k):
-            wait_gather(k)
+            wait_soon(k)
             for m in range(blocks):
-                base[:, span(m)] += down_term(m, [k])
+                base[:, span(m)] += down_term(m, [(k, soon)])
 
         @pl.loop(early, blocks)
         def _(k):
-            wait_gather(k)
+            wait_soon(k)
+
+        @pl.loop(0, blocks)
+        def _(k):
+            wait_later(k)
+
+        left = [(k, later) for k in range(early)] + [(k, soon + later) for k in range(early, blocks)]
 
         @pl.loop(0, blocks)
         def _(m):
-            finish_down(m, base[:, span(m)] + down_term(m, range(early, blocks)), odd_last)
+            finish_down(m, base[:, span(m)] + down_term(m, left), odd_last)
 
         again()
 
     @pl.when(jnp.logical_not(odd) & (z > 0))
     def _():
         base[...] = down_src[...]
-        for k in range(min(2, blocks)):
-            take(k)
+        take(0)
+        wait_soon(0)
+        if blocks > 1:
+            take(1)
 
         @pl.loop(0, blocks - 1)
         def _(k):
-            wait_gather(k)
+            @pl.when(k > 0)
+            def _():
+                wait_soon(k)
+
+            for m in range(blocks):
+                base[:, span(m)] += down_term(m, [(k, soon)])
 
             @pl.when(k + 2 < blocks)
             def _():
                 take(k + 2)
 
+            wait_later(k)
             for m in range(blocks):
-                base[:, span(m)] += down_term(m, [k])
-
-        wait_gather(blocks - 1)
+                base[:, span(m)] += down_term(m, [(k, later)])
+
+        last = blocks - 1
+        if last:
+            wait_soon(last)
         for m in range(blocks):
-            finish_down(m, base[:, span(m)] + down_term(m, [blocks - 1]), even_last)
+            base[:, span(m)] += down_term(m, [(last, soon)])
+        wait_later(last)
+        for m in range(blocks):
+            finish_down(m, base[:, span(m)] + down_term(m, [(last, later)]), even_last)
 
         again()
 
@@ -308,7 +341,7 @@
             share(h, k).start()
         acc[j, :, span(k)] += pair_in[k, 0].astype(F32)
 
-    def up(early, step):
+    def up(early):
         acc[...] = jnp.zeros_like(acc)
 
         @pl.loop(0, early)
@@ -336,19 +369,22 @@
                 i = peer(d)
                 acc[i, :, span(k)] += up_term(i, k, late)
 
-        @pl.loop(0, blocks // step)
-        def _(c):
-            for n in range(step):
-                hand_over(c * step + n)
-            for n in range(step):
-                swap(c * step + n).start()
-
-        @pl.loop(0, blocks // step)
-        def _(c):
-            for n in range(step):
-                keep(c * step + n)
-            for n in range(step):
-                combine(c * step + n)
+        ahead = min(AHEAD, blocks)
+
+        @pl.loop(0, ahead)
+        def _(k):
+            hand_over(k)
+            swap(k).start()
+
+        @pl.loop(0, blocks)
+        def _(k):
+            @pl.when(k + ahead < blocks)
+            def _():
+                hand_over(k + ahead)
+                swap(k + ahead).start()
+
+            keep(k)
+            combine(k)
 
         @pl.loop(0, blocks)
         def _(k):
@@ -359,13 +395,9 @@
         sent(pair_out, xsend)
         sent(part_out.at[:, pl.ds(0, len(halves))], psend)
 
-    @pl.when(odd & (z < layers - 1))
-    def _():
-        up(blocks // 2, 1)
-
-    @pl.when(jnp.logical_not(odd) & (z < layers - 1))
-    def _():
-        up(blocks - 1, 2)
+    @pl.when(z < layers - 1)
+    def _():
+        up(blocks // 2)
 
     @pl.when(z < layers - 1)
     def _():
@@ -411,7 +443,7 @@
             dma((blocks, groups)),
             dma(()), dma((blocks,)),
             dma(()), dma((blocks,)),
-            dma(()),
+            dma(()), dma((blocks,)),
             dma(()), dma((blocks,)),
             dma(()), dma((blocks,)),
             dma(()), dma((blocks,)),

time: 78.3 us -> 73.5 us (0.939)
  Pallas kernels: 77.5 us -> 72.7 us
    pallas_call x1, Pallas kernels: 77.5 us -> 72.7 us  [local(): pl.pallas_call(functools.partial(sweeps, layers, peers, blocks), out_shap...]
where the time goes in v3:
time: 73.5 us; the launch traced here: 73.3 us
  Pallas kernels  72.7 us (99%)
    pallas_call x1, Pallas kernels, local(): pl.pallas_call(functools.partial(sweeps, layers, peers, blocks), out_shap...  72.7 us

profile of v3, /device:TPU:0, one launch (start us, length us, event | category | flops | bytes accessed | tf_op | source)
XLA Modules:
  0.0 73.3 jit_solution(15777835365830718501)
XLA Ops:
  0.0 72.7 %shard_map.37 = f32[32,1024]{1,0:T(8,128)S(1)} custom-call(bf16[2,1024,8192]{2,1,0:T(8,128)(2,1)} %bitcast.5, f32[32,1024]{1,0:T(8,128)} %bitcast.6, f32[32,1024]{1,0:T(8,128)} %bitcast.7), custom_call_target="tpu_custom_call" | custom-call | tf_op jit(solution)/shard_map/pallas_call | solution.py:423
  72.7 0.7 copy.5
